TPU v7x, 32 devices: a whole 2x2x4 slice. The times are simulated.
32 devices in a mesh: groups: 2 (over y), band: 4 (over z), chan: 4 (over x, core).
Axes of the slice: x: 2, y: 2, z: 4, core: 2. Of those that a mesh axis runs over, the one named last changes fastest.
Arguments:
- slide_region: float32 [16, 32, 8192], P('chan', ('groups', 'band')), parts along dimension 1, may hold values from -6 to 6
- row_taps: float32 [16, 257], P('chan'), may hold values from -0.375 to 0.375
- column_taps: float32 [16, 257], replicated, may hold values from -0.375 to 0.375
- channel_mix: float32 [16, 16], replicated, may hold values from -1.5 to 1.5
Outputs:
- filtered: float32 [16, 32, 8192], P('chan', ('groups', 'band')), parts along dimension 1
There are 2 independent parts, one for each index of `groups`. A program takes and returns all parts, laid end to end along the dimension named above; an argument that names none is the same for every part. Nothing has to cross between parts.
All inputs are finite; a program needn't handle non-finite values.
Results may differ from a plain program's by a relative error of at most 0.00007.
Values sent between devices are 32-bit elements; how exact they have to be, the bound alone decides.
A program may use at most 64 MiB of HBM per device.

v0:
```python
import jax
import jax.numpy as jnp
from jax import lax
from jax.sharding import PartitionSpec as P

precise = lax.Precision.HIGHEST


def band_tables(filter_taps, tile_size):
    channels, length = filter_taps.shape
    margin = (length - 1) // 2
    period = 4 * tile_size
    border = 3 * tile_size + length
    widened = jnp.pad(filter_taps, ((0, 0), (border, border)))
    lowest = margin - tile_size + border
    window = widened[:, lowest : lowest + 3 * tile_size]
    vector = jnp.pad(window, ((0, 0), (0, tile_size)))
    repeated = jnp.tile(vector, (1, tile_size))[:, : tile_size * (period - 1)]
    toeplitz = repeated.reshape(channels, tile_size, period - 1)[:, :, : 3 * tile_size]
    stacked = jnp.transpose(toeplitz, (0, 2, 1))
    return stacked.reshape(channels, 3, tile_size, tile_size)


def along_columns(signal, filter_taps):
    tile_size = 128
    tables = band_tables(filter_taps, tile_size)
    channels, row_count, col_count = signal.shape
    tile_count = col_count // tile_size
    tiled = signal.reshape(channels, row_count, tile_count, tile_size)
    padded = jnp.pad(tiled, ((0, 0), (0, 0), (1, 1), (0, 0)))
    result = jnp.einsum(
        "crti,cij->crtj", padded[:, :, 0:tile_count], tables[:, 0], precision=precise
    )
    result = result + jnp.einsum(
        "crti,cij->crtj", padded[:, :, 1 : tile_count + 1], tables[:, 1], precision=precise
    )
    result = result + jnp.einsum(
        "crti,cij->crtj", padded[:, :, 2:], tables[:, 2], precision=precise
    )
    return result.reshape(channels, row_count, col_count)


def along_rows(signal, filter_taps):
    channels, row_count, col_count = signal.shape
    tile_size = 128 if row_count % 128 == 0 else row_count
    tables = band_tables(filter_taps, tile_size)
    tile_count = row_count // tile_size
    tiled = signal.reshape(channels, tile_count, tile_size, col_count)
    padded = jnp.pad(tiled, ((0, 0), (1, 1), (0, 0), (0, 0)))
    result = jnp.einsum("ctiw,cij->ctjw", padded[:, 0:tile_count], tables[:, 0], precision=precise)
    result = result + jnp.einsum(
        "ctiw,cij->ctjw", padded[:, 1 : tile_count + 1], tables[:, 1], precision=precise
    )
    result = result + jnp.einsum("ctiw,cij->ctjw", padded[:, 2:], tables[:, 2], precision=precise)
    return result.reshape(channels, row_count, col_count)


def on_device(slide_region, row_taps, column_taps, channel_mix):
    local_channels = slide_region.shape[0]
    across = along_columns(slide_region, row_taps)
    column_band = lax.all_to_all(across, "band", split_axis=2, concat_axis=1, tiled=True)
    first_channel = lax.axis_index("chan") * local_channels
    own_taps = lax.dynamic_slice_in_dim(column_taps, first_channel, local_channels, 0)
    vertical = along_rows(column_band, own_taps)
    own_mixing = lax.dynamic_slice_in_dim(channel_mix, first_channel, local_channels, 0)
    blended = jnp.einsum(
        "oc,chw->ohw",
        own_mixing,
        lax.all_gather(vertical, "chan", axis=0, tiled=True),
        precision=precise,
    )
    return lax.all_to_all(blended, "band", split_axis=1, concat_axis=2, tiled=True)


def solution(mesh):
    in_specs = (P("chan", ("groups", "band"), None), P("chan", None), P(), P())
    out_specs = P("chan", ("groups", "band"), None)
    return jax.shard_map(
        on_device, mesh=mesh, in_specs=in_specs, out_specs=out_specs, check_vma=False
    )
```

profile of v0, /device:TPU:0, one launch (start us, length us, event | category | flops | bytes accessed | tf_op | source)
XLA Modules:
  0.0 165.2 jit_solution(12233661536541176305)
XLA Ops:
  6.5 0.0 copy-start
  6.5 0.7 pad_slice_fusion.4
  7.3 0.1 broadcast_bitcast_fusion
  7.4 0.7 copy.47
  8.1 0.1 slice.68
  8.1 0.0 copy-start.1
  8.2 1.0 reshape.47
  9.2 0.1 slice_bitcast_fusion
  9.2 0.3 copy.24
  9.5 0.0 copy-done.1
  9.5 0.4 reshape.46
  9.9 0.6 fusion.4
  10.5 0.6 fusion.5
  11.2 0.6 fusion.3
  11.8 8.6 %copy.38 = f32[4,4,64,128]{1,0,3,2:T(4,128)} copy(f32[4,4,64,128]{3,2,1,0:T(8,128)S(1)} %fusion.3) | data formatting | bytes 1048576 | tf_op jit(solution)/shard_map/reshape | solution.py:40
  20.4 24.6 %reshape.55 = f32[4,1,32768]{2,1,0:T(1,128)} reshape(f32[8192,4,4]{2,1,0:T(4,128)} %bitcast.68) | data formatting | bytes 1048576
  45.0 6.3 %all-to-all-start = ((f32[4,1,32768]{2,1,0:T(1,128)}), f32[4,1,32768]{2,1,0:T(1,128)S(1)}, u32[]{:S(2)}, u32[]{:S(2)}) async-start(f32[4,1,32768]{2,1,0:T(1,128)} %reshape.55), calls=%async_computation | async-start | bytes 1048576 | tf_op jit(solution)/shard_map/all_to_all | solution.py:61
  51.3 0.0 all-gather.2.cloned.1.call-start
  51.3 0.8 dynamic-slice
  52.1 0.1 tile.9
  52.2 0.1 reshape.44
  52.3 0.1 reshape.45
  52.4 0.1 fusion.17
  52.5 0.4 fusion.8
  52.9 13.0 %all-to-all-done = f32[4,1,32768]{2,1,0:T(1,128)S(1)} async-done(((f32[4,1,32768]{2,1,0:T(1,128)}), f32[4,1,32768]{2,1,0:T(1,128)S(1)}, u32[]{:S(2)}, u32[]{:S(2)}) %all-to-all-start) | async-done | bytes 524320 | tf_op jit(solution)/shard_map/all_to_all | solution.py:61
  65.8 0.5 broadcast.18
  66.3 2.2 %reduce = f32[4,32768]{1,0:T(4,128)S(1)} reduce(f32[4,1,32768]{2,1,0:T(1,128)S(1)} %all-to-all-done, f32[]{:T(128)} %broadcast.18), dimensions={1}, to_apply=%all_to_all.24.reduce_sub_computation | reduce | bytes 1048580 | tf_op jit(solution)/shard_map/all_to_all | solution.py:61
  68.5 28.0 %reshape.56 = f32[8192,4,4]{2,1,0:T(4,128)} reshape(f32[4,32768]{1,0:T(4,128)S(1)} %reduce) | data formatting | bytes 1048576
  96.5 13.4 %copy.30 = f32[4,4,4,2048]{3,0,2,1:T(4,128)S(1)} copy(f32[4,4,4,2048]{2,0,3,1:T(4,128)} %bitcast.69) | data formatting | bytes 1048576 | tf_op jit(solution)/shard_map/all_to_all | solution.py:61
  109.9 0.9 convolution_add_fusion.1
  110.8 1.1 convolution_add_fusion
  111.9 0.0 all-gather.2.cloned.1.call-update
  111.9 21.8 %all-gather.2.cloned.1.call-done = f32[16,16,2048]{2,1,0:T(8,128)} async-done(((f32[4,16,2048]{2,1,0:T(8,128)}), f32[16,16,2048]{2,1,0:T(8,128)}) %all-gather.2.cloned.1.call-update) | async-done | bytes 2097168 | tf_op jit(solution)/shard_map/all_gather | solution.py:69
  133.8 0.0 copy-done
  133.8 3.8 %fusion = f32[4,16,2048]{2,0,1:T(4,128)S(1)} fusion(f32[16,16,2048]{2,1,0:T(8,128)} %all-gather.2.cloned.1.call-done, f32[16,16]{1,0:T(8,128)S(1)} %copy-done, s32[]{:T(128)S(6)} %select_n.4), kind=kOutput, calls=%fused_computation.2 | convolution fusion | flops 25165824 | bytes 2623492 | tf_op jit(solution)/shard_map/oc,chw->ohw/dot_general | solution.py:66
  137.5 19.3 %all_to_all.33 = f32[4,16,2048]{2,0,1:T(4,128)S(1)} all-to-all(f32[4,16,2048]{2,0,1:T(4,128)S(1)} %fusion), channel_id=1, replica_groups=mesh['groups'=2,'band'=4,'chan'=4] {'band'}, dimensions={1} | all-to-all | bytes 1048576 | tf_op jit(solution)/shard_map/all_to_all | solution.py:72
  156.8 0.3 copy.34
  157.2 1.2 all_to_all.30
  (4 shorter events, 0.0 us)
Async XLA Ops:
  6.5 127.2 %copy-start = (f32[16,16]{1,0:T(8,128)S(1)}, f32[16,16]{1,0:T(8,128)}, u32[]{:S(2)}) copy-start(f32[16,16]{1,0:T(8,128)} %param.7) | copy-start | bytes 3076
  8.1 1.4 copy-start.1
  45.0 20.8 %all-to-all-start = ((f32[4,1,32768]{2,1,0:T(1,128)}), f32[4,1,32768]{2,1,0:T(1,128)S(1)}, u32[]{:S(2)}, u32[]{:S(2)}) async-start(f32[4,1,32768]{2,1,0:T(1,128)} %reshape.55), calls=%async_computation | async-start | bytes 1048576 | tf_op jit(solution)/shard_map/all_to_all | solution.py:61
  51.3 82.4 %all-gather.2.cloned.1.call-start = ((), (), s32[]{:S(2)}) async-start(), calls=%async_computation.2 | async-start | bytes 2621440 | tf_op jit(solution)/shard_map/all_gather | solution.py:69
Sparse Core Ops, SparseCore 0:
  112.1 21.6 all-gather.1
where the time goes:
time: 166 us; the launch traced here: 165 us
  local copies, waits for them, and re-layouts  81.1 us (49%)
  waiting for transfers between devices  34.8 us (21%)
  blocking collectives  19.3 us (12%)
  between operations  13.5 us (8%)
  matrix products  7.99 us (5%)
  starting transfers between devices  6.35 us (4%)
  other arithmetic  2.17 us (1%)
    unnamed x8, local copies, waits for them, and re-layouts  53.4 us
    all_gather x1, waiting for transfers between devices, on_device(): lax.all_gather(vertical, 'chan', axis=0, tiled=True)  21.8 us
    all_to_all x1, blocking collectives, on_device(): lax.all_to_all(blended, 'band', split_axis=1, concat_axis=2, tiled=True)  19.3 us
    all_to_all x2, local copies, waits for them, and re-layouts, on_device(): lax.all_to_all(across, 'band', split_axis=2, concat_axis=1, tiled=True)  13.9 us
    all_to_all x1, waiting for transfers between devices, on_device(): lax.all_to_all(across, 'band', split_axis=2, concat_axis=1, tiled=True)  13 us
    reshape x1, local copies, waits for them, and re-layouts, along_columns(): return result.reshape(channels, row_count, col_count)  8.62 us
    all_to_all x1, starting transfers between devices, on_device(): lax.all_to_all(across, 'band', split_axis=2, concat_axis=1, tiled=True)  6.35 us
    dot_general x1, matrix products, on_device(): jnp.einsum('oc,chw->ohw', own_mixing, lax.all_gather(vertical, 'chan', ax...  3.77 us
  transfers between devices with their start and end apart: 2, of which 2 were waited for; matrix products, arithmetic and copies ran while one was open for 1% of the time, Pallas kernels for 0%

commit v1 on v0

--- a/solution.py
+++ b/solution.py
@@ -2,6 +2,7 @@
 import jax.numpy as jnp
 from jax import lax
 from jax.sharding import PartitionSpec as P
+from jax.lax import axis_index, axis_size, ppermute
 
 precise = lax.Precision.HIGHEST
 
@@ -63,12 +64,23 @@
     own_taps = lax.dynamic_slice_in_dim(column_taps, first_channel, local_channels, 0)
     vertical = along_rows(column_band, own_taps)
     own_mixing = lax.dynamic_slice_in_dim(channel_mix, first_channel, local_channels, 0)
-    blended = jnp.einsum(
-        "oc,chw->ohw",
-        own_mixing,
-        lax.all_gather(vertical, "chan", axis=0, tiled=True),
-        precision=precise,
-    )
+    aux = axis_size("chan")
+    then = axis_index("chan")
+    high, opened, new = (aux, then, vertical.shape[0])
+    pile = []
+    for i0 in range(high):
+        pile.append((i0, (i0 + 1) % high))
+    plain, blended = (vertical, None)
+    for j in range(high):
+        tile_out = ppermute(plain, "chan", pile) if j < high - 1 else None
+        met_up = jnp.einsum(
+            "oc,chw->ohw",
+            lax.dynamic_slice_in_dim(own_mixing, (opened - j) % high * new, plain.shape[0], axis=1),
+            plain,
+            precision=precise,
+        )
+        blended = met_up if blended is None else blended + met_up
+        plain = tile_out
     return lax.all_to_all(blended, "band", split_axis=1, concat_axis=2, tiled=True)
 
 

time: 166 us -> 151 us (0.910)
  between operations: 13.5 us -> 0.18 us
  blocking collectives: 19.3 us -> 16.5 us
    ppermute x0 -> x3, waiting for transfers between devices: none -> 21.9 us  [on_device(): tile_out = ppermute(plain, 'chan', pile) if j < high - 1 else None]
    all_gather x1 -> x0, waiting for transfers between devices: 21.8 us -> none  [on_device(): lax.all_gather(vertical, 'chan', axis=0, tiled=True)]
    all_to_all x1, blocking collectives: 19.3 us -> 16.5 us  [on_device(): lax.all_to_all(blended, 'band', split_axis=1, concat_axis=2, tiled=True)]
    dot_general x1 -> x4, matrix products: 3.77 us -> 5.18 us  [on_device(): jnp.einsum('oc,chw->ohw', lax.dynamic_slice_in_dim(own_mixing, (opened -...]
    unnamed x8 -> x6, local copies, waits for them, and re-layouts: 53.4 us -> 53.4 us
  transfers between devices with their start and end apart: 2 -> 4, of which waited for: 2 -> 4; matrix products, arithmetic and copies ran while one was open for 1% -> 4% of each run, Pallas kernels for 0% -> 0%
where the time goes in v1:
time: 151 us
  local copies, waits for them, and re-layouts  82.3 us (55%)
  waiting for transfers between devices  34.9 us (23%)
  blocking collectives  16.5 us (11%)
  matrix products  8.32 us (6%)
  starting transfers between devices  6.41 us (4%)
  other arithmetic  2.17 us (1%)
    unnamed x6, local copies, waits for them, and re-layouts  53.4 us
    ppermute x3, waiting for transfers between devices, on_device(): tile_out = ppermute(plain, 'chan', pile) if j < high - 1 else None  21.9 us
    all_to_all x1, blocking collectives, on_device(): lax.all_to_all(blended, 'band', split_axis=1, concat_axis=2, tiled=True)  16.5 us
    all_to_all x2, local copies, waits for them, and re-layouts, on_device(): lax.all_to_all(across, 'band', split_axis=2, concat_axis=1, tiled=True)  13.9 us
    all_to_all x1, waiting for transfers between devices, on_device(): lax.all_to_all(across, 'band', split_axis=2, concat_axis=1, tiled=True)  12.9 us
    reshape x1, local copies, waits for them, and re-layouts, along_columns(): return result.reshape(channels, row_count, col_count)  8.59 us
    all_to_all x1, starting transfers between devices, on_device(): lax.all_to_all(across, 'band', split_axis=2, concat_axis=1, tiled=True)  6.35 us
    dot_general x4, matrix products, on_device(): jnp.einsum('oc,chw->ohw', lax.dynamic_slice_in_dim(own_mixing, (opened -...  5.18 us
  transfers between devices with their start and end apart: 4, of which 4 were waited for; matrix products, arithmetic and copies ran while one was open for 4% of the time, Pallas kernels for 0%

profile of v1, /device:TPU:0, one launch (start us, length us, event | category | flops | bytes accessed | tf_op | source)
XLA Modules:
  0.0 150.7 jit_solution(8703117496081549901)
XLA Ops:
  0.0 0.0 copy-start
  0.0 1.4 reshape.46
  1.4 0.7 pad_slice_fusion.4
  2.1 0.1 broadcast_bitcast_fusion
  2.3 0.7 copy.48
  2.9 0.1 slice.68
  3.0 1.0 reshape.47
  4.0 0.1 slice_bitcast_fusion
  4.1 0.3 copy.26
  4.4 0.6 fusion.3
  5.0 0.6 fusion.2
  5.6 0.6 fusion.1
  6.3 8.6 %copy.41 = f32[4,4,64,128]{1,0,3,2:T(4,128)} copy(f32[4,4,64,128]{3,2,1,0:T(8,128)S(1)} %fusion.1) | data formatting | bytes 1048576 | tf_op jit(solution)/shard_map/reshape | solution.py:41
  14.8 24.6 %reshape.58 = f32[4,1,32768]{2,1,0:T(1,128)} reshape(f32[8192,4,4]{2,1,0:T(4,128)} %bitcast.75) | data formatting | bytes 1048576
  39.4 6.4 %all-to-all-start = ((f32[4,1,32768]{2,1,0:T(1,128)}), f32[4,1,32768]{2,1,0:T(1,128)S(1)}, u32[]{:S(2)}, u32[]{:S(2)}) async-start(f32[4,1,32768]{2,1,0:T(1,128)} %reshape.58), calls=%async_computation | async-start | bytes 1048576 | tf_op jit(solution)/shard_map/all_to_all | solution.py:62
  45.8 0.8 dynamic-slice
  46.6 0.1 tile.9
  46.7 0.1 reshape.44
  46.8 0.1 reshape.45
  46.9 0.1 fusion.24
  47.0 0.4 fusion.10
  47.3 12.9 %all-to-all-done = f32[4,1,32768]{2,1,0:T(1,128)S(1)} async-done(((f32[4,1,32768]{2,1,0:T(1,128)}), f32[4,1,32768]{2,1,0:T(1,128)S(1)}, u32[]{:S(2)}, u32[]{:S(2)}) %all-to-all-start) | async-done | bytes 524320 | tf_op jit(solution)/shard_map/all_to_all | solution.py:62
  60.3 0.5 broadcast.22
  60.8 2.2 %reduce = f32[4,32768]{1,0:T(4,128)S(1)} reduce(f32[4,1,32768]{2,1,0:T(1,128)S(1)} %all-to-all-done, f32[]{:T(128)} %broadcast.22), dimensions={1}, to_apply=%all_to_all.24.reduce_sub_computation | reduce | bytes 1048580 | tf_op jit(solution)/shard_map/all_to_all | solution.py:62
  63.0 28.0 %reshape.59 = f32[8192,4,4]{2,1,0:T(4,128)} reshape(f32[4,32768]{1,0:T(4,128)S(1)} %reduce) | data formatting | bytes 1048576
  91.0 13.4 %copy.31 = f32[4,4,4,2048]{3,1,2,0:T(4,128)S(1)} copy(f32[4,4,4,2048]{1,0,3,2:T(4,128)} %bitcast.76) | data formatting | bytes 1048576 | tf_op jit(solution)/shard_map/all_to_all | solution.py:62
  104.4 0.2 reshape.50
  104.6 0.6 convolution_add_fusion.4
  105.1 0.4 convolution_add_fusion.3
  105.5 0.1 collective-permute-start
  105.6 8.6 %collective-permute-done = f32[4,16,2048]{2,1,0:T(8,128)S(1)} collective-permute-done((f32[4,16,2048]{2,1,0:T(8,128)S(1)}, f32[4,16,2048]{2,1,0:T(8,128)S(1)}, u32[]{:S(2)}, u32[]{:S(2)}) %collective-permute-start) | collective-permute-done | bytes 524320 | tf_op jit(solution)/shard_map/ppermute | solution.py:75
  114.2 0.0 collective-permute-start.1
  114.2 0.0 copy-done
  114.2 1.3 fusion.7
  115.4 7.3 %collective-permute-done.1 = f32[4,16,2048]{2,1,0:T(8,128)S(1)} collective-permute-done((f32[4,16,2048]{2,1,0:T(8,128)S(1)}, f32[4,16,2048]{2,1,0:T(8,128)S(1)}, u32[]{:S(2)}, u32[]{:S(2)}) %collective-permute-start.1) | collective-permute-done | bytes 524320 | tf_op jit(solution)/shard_map/ppermute | solution.py:75
  122.8 0.0 collective-permute-start.2
  122.8 1.3 convolution_add_fusion.2
  124.1 1.3 convolution_add_fusion.1
  125.4 6.0 %collective-permute-done.2 = f32[4,16,2048]{2,1,0:T(8,128)S(1)} collective-permute-done((f32[4,16,2048]{2,1,0:T(8,128)S(1)}, f32[4,16,2048]{2,1,0:T(8,128)S(1)}, u32[]{:S(2)}, u32[]{:S(2)}) %collective-permute-start.2) | collective-permute-done | bytes 524320 | tf_op jit(solution)/shard_map/ppermute | solution.py:75
  131.4 1.3 convolution_add_fusion
  132.7 16.5 %all_to_all.33 = f32[4,16,2048]{2,0,1:T(4,128)S(1)} all-to-all(f32[4,16,2048]{2,0,1:T(4,128)S(1)} %convolution_add_fusion), channel_id=1, replica_groups=mesh['groups'=2,'band'=4,'chan'=4] {'band'}, dimensions={1} | all-to-all | bytes 1048576 | tf_op jit(solution)/shard_map/all_to_all | solution.py:84
  149.1 0.3 copy.37
  149.5 1.2 all_to_all.30
  (4 shorter events, 0.0 us)
Async XLA Ops:
  0.0 114.2 %copy-start = (f32[16,16]{1,0:T(8,128)S(1)}, f32[16,16]{1,0:T(8,128)}, u32[]{:S(2)}) copy-start(f32[16,16]{1,0:T(8,128)} %param.7) | copy-start | bytes 3076
  39.4 20.8 %all-to-all-start = ((f32[4,1,32768]{2,1,0:T(1,128)}), f32[4,1,32768]{2,1,0:T(1,128)S(1)}, u32[]{:S(2)}, u32[]{:S(2)}) async-start(f32[4,1,32768]{2,1,0:T(1,128)} %reshape.58), calls=%async_computation | async-start | bytes 1048576 | tf_op jit(solution)/shard_map/all_to_all | solution.py:62
  105.5 8.7 %collective-permute-start = (f32[4,16,2048]{2,1,0:T(8,128)S(1)}, f32[4,16,2048]{2,1,0:T(8,128)S(1)}, u32[]{:S(2)}, u32[]{:S(2)}) collective-permute-start(f32[4,16,2048]{2,1,0:T(8,128)S(1)} %convolution_add_fusion.3), channel_id=1, source_target_pairs={{0,1},{1,2},{2,3},{3,0},{4,5},{5,6},{6,7},{7,4},{8,9},{9,10},{10,1... | collective-permute-start | bytes 1572872 | tf_op jit(solution)/shard_map/ppermute | solution.py:75
  114.2 8.6 %collective-permute-start.1 = (f32[4,16,2048]{2,1,0:T(8,128)S(1)}, f32[4,16,2048]{2,1,0:T(8,128)S(1)}, u32[]{:S(2)}, u32[]{:S(2)}) collective-permute-start(f32[4,16,2048]{2,1,0:T(8,128)S(1)} %collective-permute-done), channel_id=1, source_target_pairs={{0,1},{1,2},{2,3},{3,0},{4,5},{5,6},{6,7},{7,4},{8,9},{9,10},{10,1... | collective-permute-start | bytes 1572872 | tf_op jit(solution)/shard_map/ppermute | solution.py:75
  122.8 8.6 %collective-permute-start.2 = (f32[4,16,2048]{2,1,0:T(8,128)S(1)}, f32[4,16,2048]{2,1,0:T(8,128)S(1)}, u32[]{:S(2)}, u32[]{:S(2)}) collective-permute-start(f32[4,16,2048]{2,1,0:T(8,128)S(1)} %collective-permute-done.1), channel_id=1, source_target_pairs={{0,1},{1,2},{2,3},{3,0},{4,5},{5,6},{6,7},{7,4},{8,9},{9,10},{10,1... | collective-permute-start | bytes 1572872 | tf_op jit(solution)/shard_map/ppermute | solution.py:75
